TPU v7x, 32 devices: a whole 2x2x4 slice. The times are simulated.
32 devices in a mesh: band: 8 (over z, core), grid: 4 (over y, x).
Axes of the slice: x: 2, y: 2, z: 4, core: 2. Of those that a mesh axis runs over, the one named last changes fastest.
Arguments:
- orbitals: float32 [8, 48, 2304], P('band', 'grid'), may hold values from -6 to 6
Outputs:
- compressed: float32 [8, 48, 2304], P('band', 'grid')
All inputs are finite; a program needn't handle non-finite values.
Results may differ from a plain program's by a relative error of at most 0.000092.
Values sent between devices are 32-bit elements; how exact they have to be, the bound alone decides.
A program may use at most 64 MiB of HBM per device.

v0:
```python
import functools
import math

import jax
import jax.numpy as jnp
import numpy as np
from jax import lax
from jax.experimental import pallas as pl
from jax.experimental.pallas import tpu as pltpu
from jax.sharding import PartitionSpec as P

MESH = pl.DeviceIdType.MESH
F32 = jnp.float32
BF16 = jnp.bfloat16
coulomb_scale = 50.0


def real_basis(length):
    n = np.arange(length)[:, None]
    m = np.arange(length)[None, :]
    angle = 2.0 * math.pi * ((n * np.minimum(m, length - m)) % length) / length
    table = np.where(m <= length // 2, np.cos(angle), np.sin(angle))
    weight = np.where((m == 0) | (2 * m == length), 1.0, 2.0)
    return table * np.sqrt(weight / length)


def split(value):
    high = value.astype(BF16)
    return high, (value - high.astype(F32)).astype(BF16)


def times(value, high, low, contract=((1,), (0,))):
    dims = (contract, ((), ()))
    value_high, value_low = split(value)
    dot = functools.partial(lax.dot_general, dimension_numbers=dims, preferred_element_type=F32)
    return dot(value_high, high) + (dot(value_low, high) + dot(value_high, low))


def times_left(high, low, value):
    dims = (((1,), (1,)), ((), ()))
    value_high, value_low = split(value)
    dot = functools.partial(lax.dot_general, dimension_numbers=dims, preferred_element_type=F32)
    return dot(high, value_high) + (dot(high, value_low) + dot(low, value_high))


def flat(value):
    return value.reshape(value.shape[0] * value.shape[1], value.shape[2])


def kernel(
    bands, grids, length, pieces,
    phi, tables, out,
    slabs, own, part, field, sums, exs, proj_grid, proj_band,
    dense_own, dense_part, work, coulomb, dense_field,
    sem_local, slab_send, slab_recv, fwd_send,
    own_send, own_recv, part_send, part_recv, pfwd_send, pfwd_recv,
    sum_send, sum_recv, ex_send, ex_recv, xfwd_send,
    pg_send, pg_recv, pb_send, pb_recv,
):
    b = lax.axis_index("band")
    g = lax.axis_index("grid")
    p = b // 2
    c = b % 2
    sibling = p * 2 + (1 - c)
    rows = length // grids
    pairs = bands // 2
    step = 8
    chunk = step * length
    chunks = length // step
    width = length * length // pieces
    per_piece = chunks // pieces

    def remote(src, dst, send, recv, band, grid):
        return pltpu.make_async_remote_copy(
            src_ref=src, dst_ref=dst, send_sem=send, recv_sem=recv,
            device_id=(band, grid), device_id_type=MESH,
        )

    def cut(q):
        return pl.ds(q * width, width)

    local = pltpu.make_async_copy(phi, slabs.at[b], sem_local)
    local.start()

    barrier = pltpu.get_barrier_semaphore()
    for off in range(1, bands):
        pl.semaphore_signal(barrier, inc=1, device_id=(lax.rem(b + off, bands), g), device_id_type=MESH)
    for off in range(1, grids):
        pl.semaphore_signal(barrier, inc=1, device_id=(b, lax.rem(g + off, grids)), device_id_type=MESH)

    def freq(shape, dim, base):
        m = lax.broadcasted_iota(jnp.int32, shape, dim) + base
        f = jnp.minimum(m, length - m).astype(F32)
        return f * f

    def coulomb_step(i, carry):
        shape = (step, length, length)
        squared = freq(shape, 0, i * step) + freq(shape, 1, 0) + freq(shape, 2, 0)
        coulomb[pl.ds(i * step, step)] = jnp.where(
            squared > 0.0, coulomb_scale / jnp.maximum(squared, 1.0), 0.0
        )
        return carry

    lax.fori_loop(0, chunks, coulomb_step, 0)
    local.wait()
    pl.semaphore_wait(barrier, bands + grids - 2)

    waits = []

    def go(copy):
        copy.start()
        waits.append(copy)

    for q in range(pieces):
        for off in range(1, pairs):
            peer = lax.rem(p + off, pairs) * 2 + c
            go(remote(phi.at[:, cut(q)], slabs.at[b, :, cut(q)],
                      slab_send.at[off, q], slab_recv.at[b, q], peer, g))
        for off in range(1, grids):
            go(remote(phi.at[:, cut(q)], own.at[g, :, cut(q)],
                      own_send.at[off, q], own_recv.at[g, q], b, lax.rem(g + off, grids)))
        go(remote(phi.at[:, cut(q)], slabs.at[b, :, cut(q)],
                  slab_send.at[0, q], slab_recv.at[b, q], sibling, g))

    def partner_copy(pair, q):
        return remote(
            slabs.at[pair * 2 + c, :, cut(q)], part.at[c, g, :, cut(q)],
            part_send.at[pair, q], part_recv.at[g, q], b, pair,
        )

    def to_partner(pair, q):
        @pl.when(pair != g)
        def _():
            partner_copy(pair, q).start()

    def slab_arrival(band, q):
        here = slabs.at[band, :, cut(q)]
        remote(here, here, slab_send.at[0, q], slab_recv.at[band, q], sibling, g).wait_recv()

    def pass_slabs(q):
        to_partner(p, q)
        for off in range(1, pairs):
            pair = lax.rem(p + off, pairs)
            band = pair * 2 + c
            slab_arrival(band, q)
            to_partner(pair, q)
            here = slabs.at[band, :, cut(q)]
            go(remote(here, here, fwd_send.at[off, q], slab_recv.at[band, q], sibling, g))

    def pass_partners(q):
        for off in range(1, grids):
            other = lax.rem(g + off, grids)
            here = part.at[c, other, :, cut(q)]
            remote(here, here, part_send.at[0, q], part_recv.at[other, q], b, other).wait_recv()
            go(remote(here, here, pfwd_send.at[off, q], pfwd_recv.at[other, q], sibling, g))

    def collect(q):
        slab_arrival(2 * g + 1 - c, q)
        for off in range(1, grids):
            other = lax.rem(g + off, grids)
            here = own.at[other, :, cut(q)]
            remote(here, here, own_send.at[0, q], own_recv.at[other, q], b, other).wait_recv()
            here = part.at[1 - c, other, :, cut(q)]
            remote(here, here, part_send.at[0, q], pfwd_recv.at[other, q], sibling, g).wait_recv()
        own[g, :, cut(q)] = phi[:, cut(q)]
        for k in range(2):
            part[k, g, :, cut(q)] = slabs[2 * g + k, :, cut(q)]
        for s in range(grids):
            here = slice(s * rows, (s + 1) * rows)
            dense_own[here, cut(q)] = own[s, :, cut(q)]
            for k in range(2):
                dense_part[k, here, cut(q)] = part[k, s, :, cut(q)]

    q_high, q_low, t_high, t_low = (tables[n] for n in range(4))

    def swap(value):
        return jnp.swapaxes(value, 1, 2)

    def unflat(value):
        return value.reshape(value.shape[0] // length, length, length)

    def lanes_of(i):
        return pl.ds(pl.multiple_of(i * chunk, 128), chunk)

    def stage_in(i, carry):
        lanes = lanes_of(i)
        for k in range(2):
            density = dense_own[:, lanes] * dense_part[k, :, lanes]
            first = unflat(times(density.T, q_high, q_low))
            work[k, pl.ds(i * step, step)] = unflat(times(flat(swap(first)), q_high, q_low))
        return carry

    def stage_mid(i, carry):
        here = pl.ds(pl.multiple_of(i * step, step), step)
        for k in range(2):
            value = jnp.swapaxes(work[k, :, here, :], 0, 1)
            value = unflat(times(flat(swap(value)), q_high, q_low))
            value = value * coulomb[pl.ds(i * step, step)]
            value = unflat(times(flat(value), t_high, t_low))
            work[k, :, here, :] = jnp.swapaxes(swap(value), 0, 1)
        return carry

    def send_sums(i):
        lanes = lanes_of(i)
        for off in range(1, grids):
            other = lax.rem(g + off, grids)
            remote(field.at[other, :, lanes], sums.at[g, :, lanes],
                   sum_send.at[off, i], sum_recv.at[g, i], b, other).start()

    def stage_out(i, carry):
        lanes = lanes_of(i)
        term = None
        for k in range(2):
            value = unflat(times(flat(work[k, pl.ds(i * step, step)]), t_high, t_low))
            here = dense_part[k, :, lanes] * times_left(q_high, q_low, flat(swap(value)))
            term = here if term is None else term + here
        dense_field[...] = term
        for s in range(grids):
            field[s, :, lanes] = dense_field[s * rows:(s + 1) * rows, :]

        @pl.when(i > 0)
        def _():
            send_sums(i - 1)

        return carry

    columns = [None] * bands

    def exchange_piece(q):
        for i in range(q * per_piece, (q + 1) * per_piece):
            lanes = pl.ds(i * chunk, chunk)
            for off in range(1, grids):
                other = lax.rem(g + off, grids)
                here = sums.at[other, :, lanes]
                remote(here, here, sum_send.at[0, i], sum_recv.at[other, i], b, other).wait_recv()
        value = field[g, :, cut(q)]
        for off in range(1, grids):
            value = value + sums[lax.rem(g + off, grids), :, cut(q)]
        value = -value
        exs[b, :, cut(q)] = value
        for k in range(bands):
            product = jnp.sum(slabs[k, :, cut(q)] * value, axis=0, keepdims=True)
            product = sum(product[:, n:n + 128] for n in range(0, width, 128))
            columns[k] = product if columns[k] is None else columns[k] + product
        here = exs.at[b, :, cut(q)]
        for off in range(1, pairs):
            peer = lax.rem(p + off, pairs) * 2 + c
            go(remote(here, here, ex_send.at[off, q], ex_recv.at[b, q], peer, g))
        go(remote(here, here, ex_send.at[0, q], ex_recv.at[b, q], sibling, g))

    for q in range(pieces):
        pass_slabs(q)
        if q >= 1:
            pass_partners(q - 1)
    for q in range(pieces):
        collect(q)
        lax.fori_loop(q * per_piece, (q + 1) * per_piece, stage_in, 0)
        if q == 0:
            pass_partners(pieces - 1)
    lax.fori_loop(0, chunks, stage_mid, 0)
    for q in range(pieces):
        for off in range(pairs):
            pair = lax.rem(p + off, pairs)

            @pl.when(pair != g)
            def _(pair=pair, q=q):
                slab_arrival(pair * 2 + 1 - c, q)

    for q in range(pieces):
        lax.fori_loop(q * per_piece, (q + 1) * per_piece, stage_out, 0)
    send_sums(chunks - 1)
    for q in range(pieces):
        exchange_piece(q)

    total = jnp.sum(jnp.concatenate(columns, axis=0), axis=1, keepdims=True)
    proj_grid[g] = jnp.broadcast_to(total, (bands, 128))
    for off in range(1, grids):
        other = lax.rem(g + off, grids)
        go(remote(proj_grid.at[g], proj_grid.at[g], pg_send.at[off], pg_recv.at[g], b, other))

    def ex_arrival(band, q):
        here = exs.at[band, :, cut(q)]
        remote(here, here, ex_send.at[0, q], ex_recv.at[band, q], sibling, g).wait_recv()

    def pass_exchange(q):
        for off in range(1, pairs):
            band = lax.rem(p + off, pairs) * 2 + c
            ex_arrival(band, q)
            here = exs.at[band, :, cut(q)]
            go(remote(here, here, xfwd_send.at[off, q], ex_recv.at[band, q], sibling, g))

    pass_exchange(0)
    for off in range(1, grids):
        other = lax.rem(g + off, grids)
        here = proj_grid.at[other]
        remote(here, here, pg_send.at[0], pg_recv.at[other], b, other).wait_recv()
    total = proj_grid[0]
    for s in range(1, grids):
        total = total + proj_grid[s]
    proj_band[b] = total
    for off in range(1, bands):
        other = lax.rem(b + off, bands)
        go(remote(proj_band.at[b], proj_band.at[b], pb_send.at[off], pb_recv.at[b], other, g))
    for q in range(1, pieces):
        pass_exchange(q)
    for off in range(1, bands):
        other = lax.rem(b + off, bands)
        here = proj_band.at[other]
        remote(here, here, pb_send.at[0], pb_recv.at[other], other, g).wait_recv()

    row = lax.broadcasted_iota(jnp.int32, (bands, 128), 0)
    col = lax.broadcasted_iota(jnp.int32, (bands, 128), 1)
    matrix = jnp.zeros((bands, 128), F32)
    mirrored = jnp.zeros((bands, 128), F32)
    for l in range(bands):
        entries = proj_band[l]
        matrix = jnp.where(col == l, entries, matrix)
        flipped = jnp.sum(jnp.where(row == col, entries, 0.0), axis=0, keepdims=True)
        mirrored = jnp.where(row == l, flipped, mirrored)
    definite = (matrix + mirrored) * (-0.5 / float(length**3))
    definite = jnp.where(col < bands, definite, jnp.where(col == row + bands, 1.0, 0.0))
    for j in range(bands - 1):
        line = definite[j:j + 1, :]
        ratio = definite[:, j:j + 1] / definite[j:j + 1, j:j + 1]
        definite = definite - jnp.where(row > j, ratio * line, 0.0)
    pick = jnp.sum(jnp.where(row == b, definite, 0.0), axis=0, keepdims=True)
    pivot = jnp.sum(jnp.where(col[0:1] == b, pick, 0.0), axis=1, keepdims=True)
    pick = pick / jnp.sqrt(pivot)

    for q in range(pieces):
        for off in range(pairs):
            ex_arrival(lax.rem(p + off, pairs) * 2 + (1 - c), q)
    result = jnp.zeros(phi.shape, F32)
    for l in range(bands):
        result = result + pick[:, bands + l:bands + l + 1] * exs[l]
    out[...] = result

    for copy in waits:
        copy.wait_send()
    for i in range(chunks):
        lanes = pl.ds(i * chunk, chunk)
        for off in range(1, grids):
            other = lax.rem(g + off, grids)
            remote(field.at[other, :, lanes], sums.at[g, :, lanes],
                   sum_send.at[off, i], sum_recv.at[g, i], b, other).wait_send()
    for q in range(pieces):
        for off in range(pairs):
            pair = lax.rem(p + off, pairs)

            @pl.when(pair != g)
            def _(pair=pair, q=q):
                partner_copy(pair, q).wait_send()


def per_device(bands, grids, orbitals):
    blocks, rows, cells = orbitals.shape
    length = rows * grids
    assert blocks == 1 and bands == 2 * grids and length * length == cells
    basis = real_basis(length)
    parts = []
    for table in (basis, basis.T):
        high = table.astype(np.float32).astype(BF16)
        parts += [high, (table - high.astype(np.float64)).astype(np.float32).astype(BF16)]
    tables = jnp.asarray(np.stack(parts))
    slab = (rows, cells)
    dma = lambda *n: pltpu.SemaphoreType.DMA(n)
    vmem = lambda *shape: pltpu.VMEM(shape, F32)
    pairs = bands // 2
    pieces = 3
    chunks = length // 8
    result = pl.pallas_call(
        functools.partial(kernel, bands, grids, length, pieces),
        out_shape=jax.ShapeDtypeStruct(slab, F32),
        in_specs=[pl.BlockSpec(memory_space=pltpu.VMEM)] * 2,
        out_specs=pl.BlockSpec(memory_space=pltpu.VMEM),
        scratch_shapes=[
            vmem(bands, *slab), vmem(grids, *slab), vmem(2, grids, *slab),
            vmem(grids, *slab), vmem(grids, *slab), vmem(bands, *slab),
            vmem(grids, bands, 128), vmem(bands, bands, 128),
            vmem(length, cells), vmem(2, length, cells),
            vmem(2, length, length, length), vmem(length, length, length),
            vmem(length, 8 * length),
            pltpu.SemaphoreType.DMA,
            dma(pairs, pieces), dma(bands, pieces), dma(pairs, pieces),
            dma(grids, pieces), dma(grids, pieces), dma(pairs, pieces), dma(grids, pieces),
            dma(grids, pieces), dma(grids, pieces),
            dma(grids, chunks), dma(grids, chunks),
            dma(pairs, pieces), dma(bands, pieces), dma(pairs, pieces),
            dma(grids), dma(grids), dma(bands), dma(bands),
        ],
        compiler_params=pltpu.CompilerParams(
            collective_id=0, has_side_effects=True, vmem_limit_bytes=40 * 1024 * 1024
        ),
    )(orbitals.reshape(slab), tables)
    return result.reshape(orbitals.shape)


def solution(mesh):
    bands, grids = mesh.shape["band"], mesh.shape["grid"]
    return jax.shard_map(
        functools.partial(per_device, bands, grids), mesh=mesh,
        in_specs=(P("band", "grid", None),), out_specs=P("band", "grid", None), check_vma=False,
    )
```

profile of v0, /device:TPU:0, one launch (start us, length us, event | category | flops | bytes accessed | tf_op | source)
XLA Modules:
  0.0 58.6 jit_solution(4890593687500078259)
XLA Ops:
  0.0 0.0 copy-start
  0.0 0.9 %copy.6 = f32[1,12,2304]{2,1,0:T(8,128)S(1)} copy(f32[1,12,2304]{2,0,1:T(1,128)} %param.2) | data formatting | bytes 221184
  0.9 0.0 copy-done
  0.9 56.9 %shard_map.28 = f32[12,2304]{1,0:T(8,128)S(1)} custom-call(f32[12,2304]{1,0:T(8,128)S(1)} %bitcast.5, bf16[4,48,48]{2,1,0:T(8,128)(2,1)S(1)} %copy-done), custom_call_target="tpu_custom_call" | custom-call | tf_op jit(solution)/shard_map/pallas_call | solution.py:371
  57.8 0.8 %copy.3 = f32[1,12,2304]{2,0,1:T(1,128)} copy(f32[1,12,2304]{2,1,0:T(8,128)S(1)} %bitcast.4) | data formatting | bytes 221184 | tf_op jit(solution)/shard_map/reshape | solution.py:395
Async XLA Ops:
  0.0 0.9 %copy-start = (bf16[4,48,48]{2,1,0:T(8,128)(2,1)S(1)}, bf16[4,48,48]{2,1,0:T(8,128)(2,1)}, u32[]{:S(2)}) copy-start(bf16[4,48,48]{2,1,0:T(8,128)(2,1)} %constant.2.clone.tables) | copy-start | bytes 55300
where the time goes:
time: 58.7 us; the launch traced here: 58.6 us
  Pallas kernels  56.9 us (97%)
  local copies, waits for them, and re-layouts  1.68 us (3%)
    pallas_call x1, Pallas kernels, per_device(): pl.pallas_call(functools.partial(kernel, bands, grids, length, pieces), o...  56.9 us

commit v1 on v0

--- a/solution.py
+++ b/solution.py
@@ -29,27 +29,23 @@
     return high, (value - high.astype(F32)).astype(BF16)
 
 
-def times(value, high, low, contract=((1,), (0,))):
-    dims = (contract, ((), ()))
-    value_high, value_low = split(value)
-    dot = functools.partial(lax.dot_general, dimension_numbers=dims, preferred_element_type=F32)
-    return dot(value_high, high) + (dot(value_low, high) + dot(value_high, low))
-
-
-def times_left(high, low, value):
-    dims = (((1,), (1,)), ((), ()))
-    value_high, value_low = split(value)
-    dot = functools.partial(lax.dot_general, dimension_numbers=dims, preferred_element_type=F32)
-    return dot(high, value_high) + (dot(high, value_low) + dot(low, value_high))
-
-
-def flat(value):
-    return value.reshape(value.shape[0] * value.shape[1], value.shape[2])
+def right(value, table):
+    both = jnp.concatenate(split(value), axis=1)
+    out = jnp.dot(both, table, preferred_element_type=F32)
+    half = out.shape[1] // 2
+    return out[:, :half] + out[:, half:]
+
+
+def left(table, value):
+    both = jnp.concatenate(split(value), axis=0)
+    out = jnp.dot(table, both, preferred_element_type=F32)
+    half = out.shape[0] // 2
+    return out[:half] + out[half:]
 
 
 def kernel(
     bands, grids, length, pieces,
-    phi, tables, out,
+    phi, wide, tall, out,
     slabs, own, part, field, sums, exs, proj_grid, proj_band,
     dense_own, dense_part, work, coulomb, dense_field,
     sem_local, slab_send, slab_recv, fwd_send,
@@ -88,22 +84,28 @@
     for off in range(1, grids):
         pl.semaphore_signal(barrier, inc=1, device_id=(b, lax.rem(g + off, grids)), device_id_type=MESH)
 
-    def freq(shape, dim, base):
-        m = lax.broadcasted_iota(jnp.int32, shape, dim) + base
+    def freq_of(m):
         f = jnp.minimum(m, length - m).astype(F32)
         return f * f
 
+    def freq(shape, dim, base):
+        return freq_of(lax.broadcasted_iota(jnp.int32, shape, dim) + base)
+
     def coulomb_step(i, carry):
-        shape = (step, length, length)
-        squared = freq(shape, 0, i * step) + freq(shape, 1, 0) + freq(shape, 2, 0)
+        shape = (step, length, 128)
+        lane = lax.broadcasted_iota(jnp.int32, shape, 2)
+        lane = jnp.where(lane < length, lane, lane - length)
+        squared = freq(shape, 0, i * step) + freq(shape, 1, 0) + freq_of(lane)
         coulomb[pl.ds(i * step, step)] = jnp.where(
             squared > 0.0, coulomb_scale / jnp.maximum(squared, 1.0), 0.0
         )
         return carry
 
-    lax.fori_loop(0, chunks, coulomb_step, 0)
-    local.wait()
-    pl.semaphore_wait(barrier, bands + grids - 2)
+    with jax.named_scope("coul"):
+        lax.fori_loop(0, chunks, coulomb_step, 0)
+        local.wait()
+    with jax.named_scope("barr"):
+        pl.semaphore_wait(barrier, bands + grids - 2)
 
     waits = []
 
@@ -171,33 +173,34 @@
             for k in range(2):
                 dense_part[k, here, cut(q)] = part[k, s, :, cut(q)]
 
-    q_high, q_low, t_high, t_low = (tables[n] for n in range(4))
-
-    def swap(value):
-        return jnp.swapaxes(value, 1, 2)
-
-    def unflat(value):
-        return value.reshape(value.shape[0] // length, length, length)
+    padding = jnp.zeros((128 - 2 * length, chunk), F32)
+
+    def rows_of(m):
+        return pl.ds(pl.multiple_of(m * length, 8), length)
 
     def lanes_of(i):
         return pl.ds(pl.multiple_of(i * chunk, 128), chunk)
 
     def stage_in(i, carry):
         lanes = lanes_of(i)
-        for k in range(2):
-            density = dense_own[:, lanes] * dense_part[k, :, lanes]
-            first = unflat(times(density.T, q_high, q_low))
-            work[k, pl.ds(i * step, step)] = unflat(times(flat(swap(first)), q_high, q_low))
+        mine = dense_own[:, lanes]
+        density = [mine * dense_part[k, :, lanes] for k in range(2)]
+        value = right(jnp.concatenate(density + [padding], axis=0).T, wide[0])
+        for s in range(0, step, 2):
+            two = jnp.concatenate([value[n * length:(n + 1) * length] for n in (s, s + 1)], axis=1)
+            two = left(tall[0], two)
+            for n in range(2):
+                work[rows_of(i * step + s + n), :] = two[:, n * 128:(n + 1) * 128]
         return carry
 
     def stage_mid(i, carry):
-        here = pl.ds(pl.multiple_of(i * step, step), step)
-        for k in range(2):
-            value = jnp.swapaxes(work[k, :, here, :], 0, 1)
-            value = unflat(times(flat(swap(value)), q_high, q_low))
-            value = value * coulomb[pl.ds(i * step, step)]
-            value = unflat(times(flat(value), t_high, t_low))
-            work[k, :, here, :] = jnp.swapaxes(swap(value), 0, 1)
+        for s in range(0, step, 2):
+            here = [pl.ds(i * step + s + n, length, length) for n in range(2)]
+            two = left(tall[0], jnp.concatenate([work[h, :] for h in here], axis=1))
+            two = two * jnp.concatenate([coulomb[i * step + s + n] for n in range(2)], axis=1)
+            two = left(tall[1], two)
+            for n in range(2):
+                work[here[n], :] = two[:, n * 128:(n + 1) * 128]
         return carry
 
     def send_sums(i):
@@ -209,12 +212,15 @@
 
     def stage_out(i, carry):
         lanes = lanes_of(i)
-        term = None
-        for k in range(2):
-            value = unflat(times(flat(work[k, pl.ds(i * step, step)]), t_high, t_low))
-            here = dense_part[k, :, lanes] * times_left(q_high, q_low, flat(swap(value)))
-            term = here if term is None else term + here
-        dense_field[...] = term
+        value = []
+        for s in range(0, step, 2):
+            two = jnp.concatenate([work[rows_of(i * step + s + n), :] for n in range(2)], axis=1)
+            two = left(tall[1], two)
+            value += [two[:, n * 128:(n + 1) * 128] for n in range(2)]
+        value = right(jnp.concatenate(value, axis=0), wide[1]).T
+        dense_field[...] = sum(
+            dense_part[k, :, lanes] * value[k * length:(k + 1) * length] for k in range(2)
+        )
         for s in range(grids):
             field[s, :, lanes] = dense_field[s * rows:(s + 1) * rows, :]
 
@@ -249,15 +255,21 @@
         go(remote(here, here, ex_send.at[0, q], ex_recv.at[b, q], sibling, g))
 
     for q in range(pieces):
-        pass_slabs(q)
+        with jax.named_scope(f"pslab{q}"):
+            pass_slabs(q)
         if q >= 1:
-            pass_partners(q - 1)
-    for q in range(pieces):
-        collect(q)
-        lax.fori_loop(q * per_piece, (q + 1) * per_piece, stage_in, 0)
+            with jax.named_scope(f"ppart{q-1}"):
+                pass_partners(q - 1)
+    for q in range(pieces):
+        with jax.named_scope(f"collect{q}"):
+            collect(q)
+        with jax.named_scope(f"stagein{q}"):
+            lax.fori_loop(q * per_piece, (q + 1) * per_piece, stage_in, 0, unroll=2)
         if q == 0:
-            pass_partners(pieces - 1)
-    lax.fori_loop(0, chunks, stage_mid, 0)
+            with jax.named_scope("ppartlast"):
+                pass_partners(pieces - 1)
+    with jax.named_scope("mid"):
+        lax.fori_loop(0, chunks, stage_mid, 0, unroll=6)
     for q in range(pieces):
         for off in range(pairs):
             pair = lax.rem(p + off, pairs)
@@ -266,11 +278,13 @@
             def _(pair=pair, q=q):
                 slab_arrival(pair * 2 + 1 - c, q)
 
-    for q in range(pieces):
-        lax.fori_loop(q * per_piece, (q + 1) * per_piece, stage_out, 0)
-    send_sums(chunks - 1)
-    for q in range(pieces):
-        exchange_piece(q)
+    with jax.named_scope("out"):
+        for q in range(pieces):
+            lax.fori_loop(q * per_piece, (q + 1) * per_piece, stage_out, 0, unroll=2)
+        send_sums(chunks - 1)
+    for q in range(pieces):
+        with jax.named_scope(f"exch{q}"):
+            exchange_piece(q)
 
     total = jnp.sum(jnp.concatenate(columns, axis=0), axis=1, keepdims=True)
     proj_grid[g] = jnp.broadcast_to(total, (bands, 128))
@@ -356,12 +370,22 @@
     blocks, rows, cells = orbitals.shape
     length = rows * grids
     assert blocks == 1 and bands == 2 * grids and length * length == cells
+    assert 2 * length <= 128
     basis = real_basis(length)
-    parts = []
+    wide, tall = [], []
     for table in (basis, basis.T):
-        high = table.astype(np.float32).astype(BF16)
-        parts += [high, (table - high.astype(np.float64)).astype(np.float32).astype(BF16)]
-    tables = jnp.asarray(np.stack(parts))
+        high = table.astype(np.float32).astype(BF16).astype(np.float64)
+        both = []
+        for part in (high, table - high):
+            block = np.zeros((128, 128))
+            for k in range(2):
+                here = slice(k * length, (k + 1) * length)
+                block[here, here] = part
+            both.append(block)
+        wide.append(np.tile(np.concatenate(both, axis=1), (2, 1)))
+        tall.append(np.tile(np.concatenate([high.T, (table - high).T], axis=0), (1, 2)))
+    wide = jnp.asarray(np.stack(wide).astype(BF16))
+    tall = jnp.asarray(np.stack(tall).astype(BF16))
     slab = (rows, cells)
     dma = lambda *n: pltpu.SemaphoreType.DMA(n)
     vmem = lambda *shape: pltpu.VMEM(shape, F32)
@@ -371,14 +395,14 @@
     result = pl.pallas_call(
         functools.partial(kernel, bands, grids, length, pieces),
         out_shape=jax.ShapeDtypeStruct(slab, F32),
-        in_specs=[pl.BlockSpec(memory_space=pltpu.VMEM)] * 2,
+        in_specs=[pl.BlockSpec(memory_space=pltpu.VMEM)] * 3,
         out_specs=pl.BlockSpec(memory_space=pltpu.VMEM),
         scratch_shapes=[
             vmem(bands, *slab), vmem(grids, *slab), vmem(2, grids, *slab),
             vmem(grids, *slab), vmem(grids, *slab), vmem(bands, *slab),
             vmem(grids, bands, 128), vmem(bands, bands, 128),
             vmem(length, cells), vmem(2, length, cells),
-            vmem(2, length, length, length), vmem(length, length, length),
+            vmem(length * length, 128), vmem(length, length, 128),
             vmem(length, 8 * length),
             pltpu.SemaphoreType.DMA,
             dma(pairs, pieces), dma(bands, pieces), dma(pairs, pieces),
@@ -391,7 +415,7 @@
         compiler_params=pltpu.CompilerParams(
             collective_id=0, has_side_effects=True, vmem_limit_bytes=40 * 1024 * 1024
         ),
-    )(orbitals.reshape(slab), tables)
+    )(orbitals.reshape(slab), wide, tall)
     return result.reshape(orbitals.shape)
 
 

time: 58.7 us -> 52.6 us (0.90)
  Pallas kernels: 56.9 us -> 49.7 us
  local copies, waits for them, and re-layouts: 1.68 us -> 2.63 us
    pallas_call x1, Pallas kernels: 56.9 us -> 49.7 us  [per_device(): pl.pallas_call(functools.partial(kernel, bands, grids, length, pieces), o...]
    unnamed x3 -> x5, local copies, waits for them, and re-layouts: 0.92 us -> 1.87 us
where the time goes in v1:
time: 52.6 us; the launch traced here: 52.4 us
  Pallas kernels  49.7 us (94%)
  local copies, waits for them, and re-layouts  2.63 us (5%)
    pallas_call x1, Pallas kernels, per_device(): pl.pallas_call(functools.partial(kernel, bands, grids, length, pieces), o...  49.7 us
    unnamed x5, local copies, waits for them, and re-layouts  1.87 us

profile of v1, /device:TPU:0, one launch (start us, length us, event | category | flops | bytes accessed | tf_op | source)
XLA Modules:
  0.0 52.4 jit_solution(17057414085407870424)
XLA Ops:
  0.0 0.0 copy-start.1
  0.0 0.9 %copy.7 = f32[1,12,2304]{2,1,0:T(8,128)S(1)} copy(f32[1,12,2304]{2,0,1:T(1,128)} %param.3) | data formatting | bytes 221184
  0.9 0.0 copy-done.1
  0.9 0.0 copy-start
  0.9 0.9 %copy-done = bf16[2,256,256]{2,1,0:T(8,128)(2,1)S(1)} copy-done((bf16[2,256,256]{2,1,0:T(8,128)(2,1)S(1)}, bf16[2,256,256]{2,1,0:T(8,128)(2,1)}, u32[]{:S(2)}) %copy-start) | copy-done | bytes 262168
  1.9 49.7 %shard_map.37 = f32[12,2304]{1,0:T(8,128)S(1)} custom-call(f32[12,2304]{1,0:T(8,128)S(1)} %bitcast.5, bf16[2,256,256]{2,1,0:T(8,128)(2,1)S(1)} %copy-done, bf16[2,96,96]{2,1,0:T(8,128)(2,1)S(1)} %copy-done.1), custom_call_target="tpu_custom_call" | custom-call | tf_op jit(solution)/shard_map/pallas_call | solution.py:395
  51.6 0.8 %copy.4 = f32[1,12,2304]{2,0,1:T(1,128)} copy(f32[1,12,2304]{2,1,0:T(8,128)S(1)} %bitcast.4) | data formatting | bytes 221184 | tf_op jit(solution)/shard_map/reshape | solution.py:419
Async XLA Ops:
  0.0 0.9 %copy-start.1 = (bf16[2,96,96]{2,1,0:T(8,128)(2,1)S(1)}, bf16[2,96,96]{2,1,0:T(8,128)(2,1)}, u32[]{:S(2)}) copy-start(bf16[2,96,96]{2,1,0:T(8,128)(2,1)} %constant.5.clone.tall) | copy-start | bytes 110596
  0.9 1.0 %copy-start = (bf16[2,256,256]{2,1,0:T(8,128)(2,1)S(1)}, bf16[2,256,256]{2,1,0:T(8,128)(2,1)}, u32[]{:S(2)}) copy-start(bf16[2,256,256]{2,1,0:T(8,128)(2,1)} %constant.4.clone.wide) | copy-start | bytes 786436

commit v2 on v1

v2 whole, which is shorter than its diff:
```python
import functools
import math

import jax
import jax.numpy as jnp
import numpy as np
from jax import lax
from jax.experimental import pallas as pl
from jax.experimental.pallas import tpu as pltpu
from jax.sharding import PartitionSpec as P

MESH = pl.DeviceIdType.MESH
F32 = jnp.float32
BF16 = jnp.bfloat16
coulomb_scale = 50.0
reach = 2


def real_basis(length):
    n = np.arange(length)[:, None]
    m = np.arange(length)[None, :]
    angle = 2.0 * math.pi * ((n * np.minimum(m, length - m)) % length) / length
    table = np.where(m <= length // 2, np.cos(angle), np.sin(angle))
    weight = np.where((m == 0) | (2 * m == length), 1.0, 2.0)
    return table * np.sqrt(weight / length)


def split(value):
    high = value.astype(BF16)
    return high, (value - high.astype(F32)).astype(BF16)


def right(value, table):
    both = jnp.concatenate(split(value), axis=1)
    out = jnp.dot(both, table, preferred_element_type=F32)
    half = out.shape[1] // 2
    return out[:, :half] + out[:, half:]


def left(table, value):
    both = jnp.concatenate(split(value), axis=0)
    out = jnp.dot(table, both, preferred_element_type=F32)
    half = out.shape[0] // 2
    return out[:half] + out[half:]


def kernel(
    bands, grids, length, pieces,
    phi, consts, out,
    slabs, cubes, field, sums, exs, proj_grid, proj_band,
    dense_own, dense_part, work, coulomb, dense_field, tables,
    phi_sem, own_sem, consts_sem, slab_send, slab_recv, relay_send, fwd_send, fwd_recv,
    own_send, own_recv, part_send, part_recv, pfwd_send, pfwd_recv,
    sum_send, sum_recv, ex_send, ex_recv, xrelay_send, xfwd_send,
    pg_send, pg_recv, pb_send, pb_recv,
):
    b = lax.axis_index("band")
    g = lax.axis_index("grid")
    p = b // 2
    c = b % 2
    sibling = p * 2 + (1 - c)
    rows = length // grids
    pairs = bands // 2
    step = 8
    chunk = step * length
    chunks = length // step
    width = length * length // pieces
    per_piece = chunks // pieces
    others = range(1, grids)

    def remote(src, dst, send, recv, band, grid):
        return pltpu.make_async_remote_copy(
            src_ref=src, dst_ref=dst, send_sem=send, recv_sem=recv,
            device_id=(band, grid), device_id_type=MESH,
        )

    def cut(q):
        return pl.ds(q * width, width)

    def on_line(layer):
        return (layer >= 0) & (layer < pairs)

    sent = []

    def go(make, when=None):
        if when is None:
            make().start()
        else:
            @pl.when(when)
            def _():
                make().start()
        sent.append((make, when))

    def peer(off):
        return lax.rem(g + off, grids)

    barrier = pltpu.get_barrier_semaphore()
    expected = 1 + grids - 1
    pl.semaphore_signal(barrier, inc=1, device_id=(sibling, g), device_id_type=MESH)
    for off in others:
        pl.semaphore_signal(barrier, inc=1, device_id=(b, peer(off)), device_id_type=MESH)
    for d in range(1, min(reach, pairs - 1) + 1):
        for sign in (1, -1):
            layer = p + sign * d

            @pl.when(on_line(layer))
            def _(layer=layer):
                pl.semaphore_signal(barrier, inc=1, device_id=(layer * 2 + c, g), device_id_type=MESH)

            expected = expected + on_line(layer).astype(jnp.int32)

    local = []
    for x in range(rows):
        local.append(pltpu.make_async_copy(phi.at[x], slabs.at[b, pl.ds(x, 1), :], phi_sem.at[x]))
    for x in range(rows):
        local.append(pltpu.make_async_copy(phi.at[x], cubes.at[0, g, pl.ds(x, 1), :], own_sem.at[x]))
    local.append(pltpu.make_async_copy(consts, tables, consts_sem))
    for copy in local:
        copy.start()

    def freq_of(m):
        f = jnp.minimum(m, length - m).astype(F32)
        return f * f

    def freq(shape, dim, base):
        return freq_of(lax.broadcasted_iota(jnp.int32, shape, dim) + base)

    def coulomb_step(i, carry):
        shape = (step, length, 128)
        lane = lax.broadcasted_iota(jnp.int32, shape, 2)
        lane = jnp.where(lane < length, lane, lane - length)
        squared = freq(shape, 0, i * step) + freq(shape, 1, 0) + freq_of(lane)
        coulomb[pl.ds(i * step, step)] = jnp.where(
            squared > 0.0, coulomb_scale / jnp.maximum(squared, 1.0), 0.0
        )
        return carry

    with jax.named_scope("coul"):
        lax.fori_loop(0, chunks, coulomb_step, 0)
        for copy in local:
            copy.wait()
    with jax.named_scope("barr"):
        pl.semaphore_wait(barrier, expected)

    def slab_copy(src_band, layer, q, send):
        here = slabs.at[src_band, :, cut(q)]
        return remote(here, here, send, slab_recv.at[src_band, q], layer * 2 + c, g)

    def sibling_part(s, q, src):
        return remote(src, cubes.at[1 + c, s, :, cut(q)], pfwd_send.at[s, q], pfwd_recv.at[s, q], sibling, g)

    for q in range(pieces):
        for d in range(min(reach, pairs - 1), 0, -1):
            for sign in (1, -1):
                layer = p + sign * d
                index = 2 * (d - 1) + (sign < 0)
                go(lambda layer=layer, index=index, q=q: slab_copy(b, layer, q, slab_send.at[index, q]),
                   on_line(layer))
        for off in others:
            go(lambda off=off, q=q: remote(
                slabs.at[b, :, cut(q)], cubes.at[0, g, :, cut(q)],
                own_send.at[off, q], own_recv.at[g, q], b, peer(off)))
        go(lambda q=q: sibling_part(g, q, slabs.at[b, :, cut(q)]), g == p)

    def partner_copy(layer, q):
        return remote(
            slabs.at[layer * 2 + c, :, cut(q)], cubes.at[1 + c, g, :, cut(q)],
            part_send.at[layer, q], part_recv.at[g, q], b, layer,
        )

    def take_slab(sign, d, q):
        layer = p - sign * d
        band = layer * 2 + c
        there = on_line(layer)

        @pl.when(there)
        def _():
            slab_copy(band, p, q, slab_send.at[0, q]).wait_recv()

        if d >= reach:
            way = 2 * d + (sign < 0)
            go(lambda: slab_copy(band, p + sign, q, relay_send.at[way, q]), there & on_line(p + sign))
        go(lambda: partner_copy(layer, q), there & (layer != g))
        go(lambda: sibling_part(g, q, slabs.at[band, :, cut(q)]), there & (layer == g))

    def take_part(off, q):
        other = peer(off)
        mine = cubes.at[0, other, :, cut(q)]
        remote(mine, mine, own_send.at[0, q], own_recv.at[other, q], b, other).wait_recv()
        slot = jnp.where(g == p, 0, 1 + c)

        @pl.when(g != p)
        def _():
            here = cubes.at[1 + c, other, :, cut(q)]
            remote(here, here, part_send.at[0, q], part_recv.at[other, q], b, other).wait_recv()

        go(lambda: sibling_part(other, q, cubes.at[slot, other, :, cut(q)]))

    def collect(q):
        for s in range(grids):
            here = cubes.at[2 - c, s, :, cut(q)]
            remote(here, here, pfwd_send.at[0, q], pfwd_recv.at[s, q], sibling, g).wait_recv()
        slot = jnp.where(g == p, 0, 1 + c)
        for s in range(grids):
            here = slice(s * rows, (s + 1) * rows)
            dense_own[here, cut(q)] = cubes[0, s, :, cut(q)]
            dense_part[1 - c, here, cut(q)] = cubes[2 - c, s, :, cut(q)]

            @pl.when(s != g)
            def _(s=s, here=here):
                dense_part[c, here, cut(q)] = cubes[slot, s, :, cut(q)]

            @pl.when(s == g)
            def _(s=s, here=here):
                dense_part[c, here, cut(q)] = slabs[2 * g + c, :, cut(q)]

    padding = jnp.zeros((128 - 2 * length, chunk), F32)

    def wide(n):
        return tables[n, 0:256, :]

    def tall(n):
        return tables[n, 256:256 + 2 * length, 0:2 * length]

    def rows_of(m):
        return pl.ds(pl.multiple_of(m * length, 8), length)

    def lanes_of(i):
        return pl.ds(pl.multiple_of(i * chunk, 128), chunk)

    def stage_in(i, carry):
        lanes = lanes_of(i)
        mine = dense_own[:, lanes]
        density = [mine * dense_part[k, :, lanes] for k in range(2)]
        value = right(jnp.concatenate(density + [padding], axis=0).T, wide(0))
        for s in range(0, step, 2):
            two = jnp.concatenate([value[n * length:(n + 1) * length] for n in (s, s + 1)], axis=1)
            two = left(tall(0), two)
            for n in range(2):
                work[rows_of(i * step + s + n), :] = two[:, n * 128:(n + 1) * 128]
        return carry

    def stage_mid(i, carry):
        for s in range(0, step, 2):
            here = [pl.ds(i * step + s + n, length, length) for n in range(2)]
            two = left(tall(0), jnp.concatenate([work[h, :] for h in here], axis=1))
            two = two * jnp.concatenate([coulomb[i * step + s + n] for n in range(2)], axis=1)
            two = left(tall(1), two)
            for n in range(2):
                work[here[n], :] = two[:, n * 128:(n + 1) * 128]
        return carry

    def sum_copy(i, off):
        lanes = lanes_of(i)
        other = peer(off)
        return remote(field.at[other, :, lanes], sums.at[g, :, lanes],
                      sum_send.at[off, i], sum_recv.at[g, i], b, other)

    def send_sums(i):
        for off in others:
            sum_copy(i, off).start()

    def stage_out(i, carry):
        lanes = lanes_of(i)
        value = []
        for s in range(0, step, 2):
            two = jnp.concatenate([work[rows_of(i * step + s + n), :] for n in range(2)], axis=1)
            two = left(tall(1), two)
            value += [two[:, n * 128:(n + 1) * 128] for n in range(2)]
        value = right(jnp.concatenate(value, axis=0), wide(1)).T
        dense_field[...] = sum(
            dense_part[k, :, lanes] * value[k * length:(k + 1) * length] for k in range(2)
        )
        for s in range(grids):
            field[s, :, lanes] = dense_field[s * rows:(s + 1) * rows, :]

        @pl.when(i > 0)
        def _():
            send_sums(i - 1)

        return carry

    columns = [None] * bands

    def ex_copy(src_band, band, q, send):
        here = exs.at[src_band, :, cut(q)]
        return remote(here, here, send, ex_recv.at[src_band, q], band, g)

    def exchange_piece(q):
        for i in range(q * per_piece, (q + 1) * per_piece):
            lanes = pl.ds(i * chunk, chunk)
            for off in others:
                other = peer(off)
                here = sums.at[other, :, lanes]
                remote(here, here, sum_send.at[0, i], sum_recv.at[other, i], b, other).wait_recv()
        value = field[g, :, cut(q)]
        for off in others:
            value = value + sums[peer(off), :, cut(q)]
        value = -value
        exs[b, :, cut(q)] = value
        for d in range(min(reach, pairs - 1), 0, -1):
            go(lambda d=d: ex_copy(b, (p + d) * 2 + c, q, ex_send.at[d, q]), on_line(p + d))
        go(lambda: ex_copy(b, sibling, q, ex_send.at[0, q]), c == 0)
        for k in range(bands):
            product = jnp.sum(slabs[k, :, cut(q)] * value, axis=0, keepdims=True)
            product = sum(product[:, n:n + 128] for n in range(0, width, 128))
            columns[k] = product if columns[k] is None else columns[k] + product

    near = range(1, min(reach, pairs - 1) + 1)
    far = range(reach + 1, pairs)
    with jax.named_scope("slabnear"):
        for q in range(pieces):
            for d in near:
                for sign in (1, -1):
                    take_slab(sign, d, q)
    with jax.named_scope("slabfar"):
        for d in far:
            for q in range(pieces):
                for sign in (1, -1):
                    take_slab(sign, d, q)
    for q in range(pieces):
        with jax.named_scope(f"part{q}"):
            for off in others:
                take_part(off, q)
        if q >= 1:
            with jax.named_scope(f"collect{q-1}"):
                collect(q - 1)
            with jax.named_scope(f"stagein{q-1}"):
                lax.fori_loop((q - 1) * per_piece, q * per_piece, stage_in, 0, unroll=True)
    with jax.named_scope("collectlast"):
        collect(pieces - 1)
    with jax.named_scope("stageinlast"):
        lax.fori_loop((pieces - 1) * per_piece, chunks, stage_in, 0, unroll=True)

    def whole_slab(band):
        here = slabs.at[band]
        return remote(here, here, fwd_send.at[band], fwd_recv.at[band], sibling, g)

    for s in range(pairs):
        go(lambda s=s: whole_slab(2 * s + c))
    with jax.named_scope("mid"):
        lax.fori_loop(0, chunks, stage_mid, 0, unroll=True)
    with jax.named_scope("out"):
        for q in range(pieces):
            lax.fori_loop(q * per_piece, (q + 1) * per_piece, stage_out, 0, unroll=True)
        send_sums(chunks - 1)
        for s in range(pairs):
            whole_slab(2 * s + 1 - c).wait_recv()
    for q in range(pieces):
        with jax.named_scope(f"exch{q}"):
            exchange_piece(q)

    total = jnp.sum(jnp.concatenate(columns, axis=0), axis=1, keepdims=True)
    proj_grid[g] = jnp.broadcast_to(total, (bands, 128))
    for off in others:
        go(lambda off=off: remote(proj_grid.at[g], proj_grid.at[g], pg_send.at[off], pg_recv.at[g], b, peer(off)))

    def take_exchange(d, q):
        layer = p - d
        band = layer * 2 + c
        there = layer >= 0

        @pl.when(there)
        def _():
            ex_copy(band, b, q, ex_send.at[0, q]).wait_recv()

        if d >= reach:
            go(lambda: ex_copy(band, (p + 1) * 2 + c, q, xrelay_send.at[d, q]), there & on_line(p + 1))
        go(lambda: ex_copy(band, sibling, q, xfwd_send.at[d, q]), there)

    with jax.named_scope("pex0"):
        for d in near:
            take_exchange(d, 0)
    with jax.named_scope("projgrid"):
        for off in others:
            other = peer(off)
            here = proj_grid.at[other]
            remote(here, here, pg_send.at[0], pg_recv.at[other], b, other).wait_recv()
        total = proj_grid[0]
        for s in range(1, grids):
            total = total + proj_grid[s]
        proj_band[b] = total
    for off in range(1, bands):
        go(lambda off=off: remote(
            proj_band.at[b], proj_band.at[b], pb_send.at[off], pb_recv.at[b], b + off, g), b + off < bands)
    with jax.named_scope("pexnear"):
        for q in range(1, pieces):
            for d in near:
                take_exchange(d, q)
    with jax.named_scope("pexfar"):
        for d in far:
            for q in range(pieces):
                take_exchange(d, q)
    with jax.named_scope("projband"):
        for l in range(bands - 1):
            @pl.when(l < b)
            def _(l=l):
                here = proj_band.at[l]
                remote(here, here, pb_send.at[0], pb_recv.at[l], l, g).wait_recv()

    row = lax.broadcasted_iota(jnp.int32, (bands, 128), 0)
    col = lax.broadcasted_iota(jnp.int32, (bands, 128), 1)
    matrix = jnp.zeros((bands, 128), F32)
    mirrored = jnp.zeros((bands, 128), F32)
    for l in range(bands):
        entries = proj_band[l]
        matrix = jnp.where(col == l, entries, matrix)
        flipped = jnp.sum(jnp.where(row == col, entries, 0.0), axis=0, keepdims=True)
        mirrored = jnp.where(row == l, flipped, mirrored)
    definite = (matrix + mirrored) * (-0.5 / float(length**3))
    unit = (col == row) | (col == row + bands)
    definite = jnp.where((row <= b) & (col <= b), definite, jnp.where(unit, 1.0, 0.0))
    for j in range(bands - 1):
        line = definite[j:j + 1, :]
        ratio = definite[:, j:j + 1] / definite[j:j + 1, j:j + 1]
        definite = definite - jnp.where(row > j, ratio * line, 0.0)
    pick = jnp.sum(jnp.where(row == b, definite, 0.0), axis=0, keepdims=True)
    pivot = jnp.sum(jnp.where(col[0:1] == b, pick, 0.0), axis=1, keepdims=True)
    pick = pick / jnp.sqrt(pivot)

    with jax.named_scope("final"):
        for q in range(pieces):
            for d in range(pairs):
                layer = p - d

                @pl.when((layer >= 0) if d > 0 else (c == 1))
                def _(layer=layer):
                    ex_copy(layer * 2 + 1 - c, b, q, ex_send.at[0, q]).wait_recv()

            result = jnp.zeros((rows, width), F32)
            for l in range(bands):
                result = result + pick[:, bands + l:bands + l + 1] * jnp.where(l <= b, exs[l, :, cut(q)], 0.0)
            out[:, 0, cut(q)] = result

    with jax.named_scope("drain"):
        for make, when in sent:
            if when is None:
                make().wait_send()
            else:
                @pl.when(when)
                def _(make=make):
                    make().wait_send()
        for i in range(chunks):
            for off in others:
                sum_copy(i, off).wait_send()


def per_device(bands, grids, orbitals):
    blocks, rows, cells = orbitals.shape
    length = rows * grids
    assert blocks == 1 and bands == 2 * grids and length * length == cells
    assert 2 * length <= 128
    basis = real_basis(length)
    consts = np.zeros((2, 256 + 2 * length, 256))
    for n, table in enumerate((basis, basis.T)):
        high = table.astype(np.float32).astype(BF16).astype(np.float64)
        for m, part in enumerate((high, table - high)):
            for k in range(4):
                r = 128 * (k // 2) + (k % 2) * length
                s = 128 * m + (k % 2) * length
                consts[n, r:r + length, s:s + length] = part
            for k in range(2):
                consts[n, 256 + m * length:256 + (m + 1) * length, k * length:(k + 1) * length] = part.T
    consts = jnp.asarray(consts.astype(BF16))
    slab = (rows, cells)
    dma = lambda *n: pltpu.SemaphoreType.DMA(n)
    vmem = lambda *shape: pltpu.VMEM(shape, F32)
    pairs = bands // 2
    pieces = 3
    chunks = length // 8
    result = pl.pallas_call(
        functools.partial(kernel, bands, grids, length, pieces),
        out_shape=jax.ShapeDtypeStruct((rows, 1, cells), F32),
        in_specs=[pl.BlockSpec(memory_space=pltpu.HBM)] * 2,
        out_specs=pl.BlockSpec(memory_space=pltpu.VMEM),
        scratch_shapes=[
            vmem(bands, *slab), vmem(3, grids, *slab),
            vmem(grids, *slab), vmem(grids, *slab), vmem(bands, *slab),
            vmem(grids, bands, 128), vmem(bands, bands, 128),
            vmem(length, cells), vmem(2, length, cells),
            vmem(length * length, 128), vmem(length, length, 128),
            vmem(length, 8 * length), pltpu.VMEM(consts.shape, BF16),
            dma(rows), dma(rows), pltpu.SemaphoreType.DMA,
            dma(2 * reach, pieces), dma(bands, pieces), dma(2 * pairs, pieces), dma(bands), dma(bands),
            dma(grids, pieces), dma(grids, pieces), dma(pairs, pieces), dma(grids, pieces),
            dma(grids, pieces), dma(grids, pieces),
            dma(grids, chunks), dma(grids, chunks),
            dma(reach + 1, pieces), dma(bands, pieces), dma(pairs, pieces), dma(pairs, pieces),
            dma(grids), dma(grids), dma(bands), dma(bands),
        ],
        compiler_params=pltpu.CompilerParams(
            collective_id=0, has_side_effects=True, vmem_limit_bytes=40 * 1024 * 1024
        ),
    )(orbitals.reshape(rows, 1, cells), consts)
    return result.reshape(orbitals.shape)


def solution(mesh):
    bands, grids = mesh.shape["band"], mesh.shape["grid"]
    return jax.shard_map(
        functools.partial(per_device, bands, grids), mesh=mesh,
        in_specs=(P("band", "grid", None),), out_specs=P("band", "grid", None), check_vma=False,
    )
```

time: 52.6 us -> 46.2 us (0.88)
  the two profiles are of different devices: /device:TPU:0 before, /device:TPU:25 now
where the time goes in v2:
time: 46.2 us; the launch traced here: 46.1 us
  Pallas kernels  43.5 us (94%)
  local copies, waits for them, and re-layouts  2.53 us (5%)
    pallas_call x1, Pallas kernels, per_device(): pl.pallas_call(functools.partial(kernel, bands, grids, length, pieces), o...  43.5 us
    unnamed x5, local copies, waits for them, and re-layouts  2.53 us

profile of v2, /device:TPU:25, one launch (start us, length us, event | category | flops | bytes accessed | tf_op | source)
XLA Modules:
  0.0 46.1 jit_solution(7839114004245795557)
XLA Ops:
  0.0 0.0 copy-start
  0.0 1.0 %copy-done = bf16[2,352,256]{2,1,0:T(8,128)(2,1)S(1)} copy-done((bf16[2,352,256]{2,1,0:T(8,128)(2,1)S(1)}, bf16[2,352,256]{2,1,0:T(8,128)(2,1)}, u32[]{:S(2)}) %copy-start) | copy-done | bytes 360472
  1.0 0.0 copy-start.1
  1.0 0.9 %copy-done.1 = f32[1,12,2304]{2,0,1:T(1,128)S(1)} copy-done((f32[1,12,2304]{2,0,1:T(1,128)S(1)}, f32[1,12,2304]{2,0,1:T(1,128)}, u32[]{:S(2)}) %copy-start.1) | copy-done | bytes 110616
  1.9 43.5 %shard_map.28 = f32[12,1,2304]{2,1,0:T(1,128)S(1)} custom-call(f32[12,1,2304]{2,1,0:T(1,128)S(1)} %bitcast.3, bf16[2,352,256]{2,1,0:T(8,128)(2,1)S(1)} %copy-done), custom_call_target="tpu_custom_call" | custom-call | tf_op jit(solution)/shard_map/pallas_call | solution.py:471
  45.4 0.6 %copy.4 = f32[1,12,2304]{2,0,1:T(1,128)} copy(f32[1,12,2304]{2,0,1:T(1,128)S(1)} %bitcast.2) | data formatting | bytes 221184
Async XLA Ops:
  0.0 1.0 %copy-start = (bf16[2,352,256]{2,1,0:T(8,128)(2,1)S(1)}, bf16[2,352,256]{2,1,0:T(8,128)(2,1)}, u32[]{:S(2)}) copy-start(bf16[2,352,256]{2,1,0:T(8,128)(2,1)} %constant.2.clone.consts) | copy-start | bytes 1081348
  1.0 0.9 %copy-start.1 = (f32[1,12,2304]{2,0,1:T(1,128)S(1)}, f32[1,12,2304]{2,0,1:T(1,128)}, u32[]{:S(2)}) copy-start(f32[1,12,2304]{2,0,1:T(1,128)} %param.2) | copy-start | bytes 331780

commit v3 on v2

--- a/solution.py
+++ b/solution.py
@@ -491,7 +491,7 @@
         compiler_params=pltpu.CompilerParams(
             collective_id=0, has_side_effects=True, vmem_limit_bytes=40 * 1024 * 1024
         ),
-    )(orbitals.reshape(rows, 1, cells), consts)
+    )(*(pltpu.with_memory_space_constraint(a, pltpu.HBM) for a in (orbitals.reshape(rows, 1, cells), consts)))
     return result.reshape(orbitals.shape)
 
 

time: 46.2 us -> 44.4 us (0.961)
  local copies, waits for them, and re-layouts: 2.53 us -> 0.65 us
    unnamed x5 -> x1, local copies, waits for them, and re-layouts: 2.53 us -> 0.65 us
where the time goes in v3:
time: 44.4 us; the launch traced here: 44.2 us
  Pallas kernels  43.5 us (98%)
  local copies, waits for them, and re-layouts  0.65 us (1%)
    pallas_call x1, Pallas kernels, per_device(): pl.pallas_call(functools.partial(kernel, bands, grids, length, pieces), o...  43.5 us

profile of v3, /device:TPU:25, one launch (start us, length us, event | category | flops | bytes accessed | tf_op | source)
XLA Modules:
  0.0 44.2 jit_solution(11549941845821256571)
XLA Ops:
  0.0 43.5 %shard_map.28 = f32[12,1,2304]{2,1,0:T(1,128)S(1)} custom-call(f32[12,1,2304]{2,1,0:T(1,128)} %bitcast.3, bf16[2,352,256]{2,1,0:T(8,128)(2,1)} %constant.2.clone.consts), custom_call_target="tpu_custom_call" | custom-call | tf_op jit(solution)/shard_map/pallas_call | solution.py:471
  43.6 0.6 %copy.4 = f32[1,12,2304]{2,0,1:T(1,128)} copy(f32[1,12,2304]{2,0,1:T(1,128)S(1)} %bitcast.2) | data formatting | bytes 221184
